TPU v7x, 32 devices: a whole 2x2x4 slice. The times are simulated.
32 devices in a mesh: pts: 8 (over z, y), hrs: 4 (over x, core).
Axes of the slice: x: 2, y: 2, z: 4, core: 2. Of those that a mesh axis runs over, the one named last changes fastest.
Arguments:
- fields: float32 [512, 65536], P(('pts', 'hrs')), may hold values from -2000 to 2000, as said below
- probes: float32 [256, 512], replicated, may hold values from -0.25 to 0.25
Outputs:
- basis_rows: float32 [256, 65536], P(None, ('pts', 'hrs'))
- coeffs: float32 [256, 512], replicated
Inputs may be any that keep to these rules, and one draw needn't show every extreme that they name: `fields`: every hour and every grid point carries its own scale, and the values are real-valued and never all zero.
All inputs are finite; a program needn't handle non-finite values.
Results may differ from a plain program's by a relative error of at most 0.00017.
Values sent between devices are 32-bit elements; how exact they have to be, the bound alone decides.
A program may use at most 64 MiB of HBM per device.

v0:
```python
import jax
import jax.numpy as jnp
from jax import lax
from jax.sharding import PartitionSpec as P

highest = lax.Precision.HIGHEST


def contract_last(left, right):
    return lax.dot_general(
        left, right, (((1,), (1,)), ((), ())), precision=highest, preferred_element_type=jnp.float32
    )


def on_device(fields, probes):
    n_pts = lax.axis_size("pts")
    n_hrs = lax.axis_size("hrs")
    panels = lax.all_to_all(fields, ("pts", "hrs"), split_axis=1, concat_axis=0, tiled=True)
    n_points = panels.shape[1] * n_pts * n_hrs
    sketched = jnp.dot(probes, panels, precision=highest, preferred_element_type=jnp.float32)
    cross_sum = lax.psum(contract_last(sketched, panels) / n_points, ("pts", "hrs"))
    local_gram = contract_last(sketched, sketched) / n_points
    gram_sum = lax.psum(local_gram, ("pts", "hrs"))
    factor = jnp.linalg.cholesky(gram_sum)
    basis_rows = lax.linalg.triangular_solve(factor, sketched, left_side=True, lower=True)
    coeffs = lax.linalg.triangular_solve(factor, cross_sum, left_side=True, lower=True)
    return (basis_rows, coeffs)


def solution(mesh):
    return jax.shard_map(
        on_device,
        mesh=mesh,
        in_specs=(P(("pts", "hrs"), None), P()),
        out_specs=(P(None, ("pts", "hrs")), P()),
        check_vma=False,
    )
```

profile of v0, /device:TPU:0, one launch (start us, length us, event | category | flops | bytes accessed | tf_op | source)
XLA Modules:
  0.0 328.4 jit_solution(12238962326394786213)
XLA Ops:
  7.2 0.0 copy-start
  7.2 0.0 all-reduce.4.cloned.1.call-start
  7.2 2.5 copy.17
  9.7 100.7 %all_to_all.19 = f32[16,32,2048]{2,0,1:T(8,128)S(1)} all-to-all(f32[16,32,2048]{2,0,1:T(8,128)S(1)} %bitcast.50), channel_id=1, replica_groups=mesh['pts'=8,'hrs'=4] {'pts','hrs'}, dimensions={1} | all-to-all | bytes 8388608 | tf_op jit(solution)/shard_map/all_to_all | solution.py:18
  110.5 3.7 %fusion.13 = f32[256,2048]{1,0:T(8,128)S(1)} fusion(f32[256,512]{1,0:T(8,128)S(1)} %copy-done, f32[512,2048]{1,0:T(8,128)S(1)} %bitcast.48), kind=kOutput, calls=%fused_computation.38 | convolution fusion | flops 3221225472 | bytes 6815744 | tf_op jit(solution)/shard_map/dot_general | solution.py:20
  114.2 4.5 %convolution_multiply_fusion = f32[256,512]{1,0:T(8,128)} fusion(f32[256,2048]{1,0:T(8,128)S(1)} %fusion.13, f32[512,2048]{1,0:T(8,128)S(1)} %bitcast.49), kind=kOutput, calls=%fused_computation.5 | convolution fusion | flops 3221356544 | bytes 6815744 | tf_op jit(solution)/shard_map/dot_general | solution.py:10
  118.7 2.6 convolution_multiply_fusion.1
  121.3 0.0 all-reduce.4.cloned.1.call-update
  121.3 129.5 %all-reduce.4.cloned.1.call-done = (f32[256,256]{0,1:T(8,128)}, f32[256,512]{1,0:T(8,128)}) async-done(((f32[256,256]{0,1:T(8,128)}, f32[256,512]{1,0:T(8,128)}), (f32[256,256]{0,1:T(8,128)}, f32[256,512]{1,0:T(8,128)})) %all-reduce.4.cloned.1.call-update) | async-done | bytes 786448 | tf_op jit(solution)/shard_map/psum | solution.py:23
  250.9 1.1 copy.13
  252.0 1.0 fusion.4
  253.0 11.9 %cholesky.50 = f32[128,128]{1,0:T(8,128)S(1)} custom-call(f32[128,128]{1,0:T(8,128)S(1)} %cholesky.118), custom_call_target="Cholesky" | custom-call | tf_op jit(solution)/shard_map/jit(cholesky)/cholesky | solution.py:24
  264.9 9.8 %custom-call.16 = f32[1,128,128]{1,2,0:T(8,128)S(1)} custom-call(f32[1,128,128]{2,1,0:T(8,128)S(1)} %get-tuple-element.25), custom_call_target="InvertDiagBlocksLowerTriangular" | custom-call | tf_op jit(solution)/shard_map/jit(cholesky)/cholesky | solution.py:24
  274.7 0.2 constant_dynamic-update-slice_fusion.1
  274.9 0.3 convolution_subtract_fusion.2
  275.2 11.7 %cholesky.105 = f32[128,128]{1,0:T(8,128)S(1)} custom-call(f32[128,128]{1,0:T(8,128)S(1)} %convolution_subtract_fusion.2), custom_call_target="Cholesky" | custom-call | tf_op jit(solution)/shard_map/jit(cholesky)/cholesky | solution.py:24
  287.0 0.6 compare_reduce_fusion
  288.9 0.1 triangular_solve.72
  289.0 4.0 %while.1 = (s32[]{:T(128)}, f32[256,256]{1,0:T(8,128)S(1)}, s32[2,2]{1,0:T(2,128)S(1)}, f32[2,128,128]{2,1,0:T(8,128)S(1)}, s32[]{:T(128)}) while((s32[]{:T(128)}, f32[256,256]{1,0:T(8,128)S(1)}, s32[2,2]{1,0:T(2,128)S(1)}, f32[2,128,128]{2,1,0:T(8,128)S(1)}, s32[]{:T(128)}) %tuple.27), condition=%wide.while_cond, body=%wide.while_body.sunk | while | flops 2 | bytes 131181 | solution.py:25
  289.0 0.6 fusion.27
  289.6 1.4 bitcast_dynamic-update-slice_fusion.2
  291.0 0.6 fusion.27
  291.6 1.4 bitcast_dynamic-update-slice_fusion.2
  293.0 19.9 %custom-call.17 = f32[2,128,128]{1,2,0:T(8,128)S(1)} custom-call(f32[2,128,128]{2,1,0:T(8,128)S(1)} %get-tuple-element.9), custom_call_target="InvertDiagBlocksLowerTriangular" | custom-call | tf_op jit(solution)/shard_map/triangular_solve | solution.py:25
  312.9 1.1 fusion
  314.0 1.4 fusion.2
  315.3 1.3 convolution_subtract_fusion.1
  316.7 0.4 fusion.8
  317.1 0.8 pad_maximum_fusion.1
  317.9 1.0 convolution_subtract_fusion
  319.0 1.0 fusion.9
  320.0 1.5 pad_maximum_fusion
  (10 shorter events, 0.2 us)
Async XLA Ops:
  7.2 103.3 %copy-start = (f32[256,512]{1,0:T(8,128)S(1)}, f32[256,512]{1,0:T(8,128)}, u32[]{:S(2)}) copy-start(f32[256,512]{1,0:T(8,128)} %param.3) | copy-start | bytes 1572868
  7.2 243.7 %all-reduce.4.cloned.1.call-start = ((), (), s32[]{:S(2)}) async-start(), calls=%async_computation.1 | async-start | bytes 1572864 | tf_op jit(solution)/shard_map/psum | solution.py:23
Sparse Core Ops, SparseCore 0:
  121.4 129.3 all-reduce.3
where the time goes:
time: 329 us; the launch traced here: 328 us
  waiting for transfers between devices  130 us (40%)
  blocking collectives  101 us (31%)
  other arithmetic  57.4 us (17%)
  matrix products  17.5 us (5%)
  between operations  15.5 us (5%)
  local copies, waits for them, and re-layouts  7.64 us (2%)
    psum x1, waiting for transfers between devices, on_device(): gram_sum = lax.psum(local_gram, ('pts', 'hrs'))  130 us
    all_to_all x1, blocking collectives, on_device(): lax.all_to_all(fields, ('pts', 'hrs'), split_axis=1, concat_axis=0, tiled...  101 us
    another operation x6, other arithmetic, on_device(): factor = jnp.linalg.cholesky(gram_sum)  34.1 us
    another operation x4, other arithmetic, on_device(): lax.linalg.triangular_solve(factor, sketched, left_side=True, lower=True)  21.5 us
    dot_general x2, matrix products, contract_last(): lax.dot_general(left, right, (((1,), (1,)), ((), ())), precision=highest,...  7.09 us
  transfers between devices with their start and end apart: 1, of which 1 were waited for; matrix products, arithmetic and copies ran while one was open for 0% of the time, Pallas kernels for 0%

commit v1 on v0

--- a/solution.py
+++ b/solution.py
@@ -20,7 +20,8 @@
     sketched = jnp.dot(probes, panels, precision=highest, preferred_element_type=jnp.float32)
     cross_sum = lax.psum(contract_last(sketched, panels) / n_points, ("pts", "hrs"))
     local_gram = contract_last(sketched, sketched) / n_points
-    gram_sum = lax.psum(local_gram, ("pts", "hrs"))
+    pack_the_packet = lambda my_tile: lax.all_gather(my_tile, axis_name=("pts", "hrs")).sum(axis=0)
+    gram_sum = pack_the_packet(local_gram)
     factor = jnp.linalg.cholesky(gram_sum)
     basis_rows = lax.linalg.triangular_solve(factor, sketched, left_side=True, lower=True)
     coeffs = lax.linalg.triangular_solve(factor, cross_sum, left_side=True, lower=True)

time: 329 us -> 342 us (1.040)
  waiting for transfers between devices: 130 us -> 138 us
    all_gather x0 -> x1, waiting for transfers between devices: none -> 69.3 us  [on_device(): lax.all_gather(my_tile, axis_name=('pts', 'hrs')).sum(axis=0)]
    psum x1, waiting for transfers between devices: 130 us -> 68.4 us  [on_device(): lax.psum(contract_last(sketched, panels) / n_points, ('pts', 'hrs'))]
    reduce_sum x0 -> x1, other arithmetic: none -> 3.93 us  [on_device(): lax.all_gather(my_tile, axis_name=('pts', 'hrs')).sum(axis=0)]
  transfers between devices with their start and end apart: 1 -> 2, of which waited for: 1 -> 2; matrix products, arithmetic and copies ran while one was open for 0% -> 21% of each run, Pallas kernels for 0% -> 0%
where the time goes in v1:
time: 342 us
  waiting for transfers between devices  138 us (40%)
  blocking collectives  101 us (30%)
  other arithmetic  60.2 us (18%)
  matrix products  20.7 us (6%)
  between operations  15.5 us (5%)
  local copies, waits for them, and re-layouts  6.69 us (2%)
    all_to_all x1, blocking collectives, on_device(): lax.all_to_all(fields, ('pts', 'hrs'), split_axis=1, concat_axis=0, tiled...  101 us
    all_gather x1, waiting for transfers between devices, on_device(): lax.all_gather(my_tile, axis_name=('pts', 'hrs')).sum(axis=0)  69.3 us
    psum x1, waiting for transfers between devices, on_device(): lax.psum(contract_last(sketched, panels) / n_points, ('pts', 'hrs'))  68.4 us
    another operation x6, other arithmetic, on_device(): factor = jnp.linalg.cholesky(gram_sum)  34.2 us
    another operation x4, other arithmetic, on_device(): lax.linalg.triangular_solve(factor, sketched, left_side=True, lower=True)  21.2 us
    dot_general x2, matrix products, contract_last(): lax.dot_general(left, right, (((1,), (1,)), ((), ())), precision=highest,...  9.24 us
  transfers between devices with their start and end apart: 2, of which 2 were waited for; matrix products, arithmetic and copies ran while one was open for 21% of the time, Pallas kernels for 0%

profile of v1, /device:TPU:0, one launch (start us, length us, event | category | flops | bytes accessed | tf_op | source)
XLA Modules:
  0.0 341.9 jit_solution(9663236041237582199)
XLA Ops:
  7.2 0.0 all-gather.3.cloned.1.call-start
  7.2 2.5 copy.12
  9.7 100.7 %all_to_all.19 = f32[16,32,2048]{2,0,1:T(8,128)S(1)} all-to-all(f32[16,32,2048]{2,0,1:T(8,128)S(1)} %bitcast.51), channel_id=1, replica_groups=mesh['pts'=8,'hrs'=4] {'pts','hrs'}, dimensions={1} | all-to-all | bytes 8388608 | tf_op jit(solution)/shard_map/all_to_all | solution.py:18
  110.5 3.7 %fusion.13 = f32[256,2048]{1,0:T(8,128)S(1)} fusion(f32[256,512]{1,0:T(8,128)S(1)} %copy-done, f32[512,2048]{1,0:T(8,128)S(1)} %bitcast.49), kind=kOutput, calls=%fused_computation.38 | convolution fusion | flops 3221225472 | bytes 6815744 | tf_op jit(solution)/shard_map/dot_general | solution.py:20
  114.2 2.6 convolution_multiply_fusion.1
  116.8 0.2 all-reduce.3.cloned.1.call-start
  117.1 6.7 %convolution_multiply_fusion = f32[256,512]{1,0:T(8,128)} fusion(f32[256,2048]{1,0:T(8,128)S(1)} %fusion.13, f32[512,2048]{1,0:T(8,128)} %bitcast.50), kind=kOutput, calls=%fused_computation.5 | convolution fusion | flops 3221356544 | bytes 6815744 | tf_op jit(solution)/shard_map/dot_general | solution.py:10
  123.7 69.3 %all-gather.3.cloned.1.call-done = f32[8192,256]{1,0:T(8,128)} async-done(((f32[256,256]{1,0:T(8,128)}), f32[8192,256]{1,0:T(8,128)}) %all-gather.3.cloned.1.call-update) | async-done | bytes 8388624 | tf_op jit(solution)/shard_map/all_gather | solution.py:23
  193.1 3.9 %reduce_sum.9 = f32[256,256]{1,0:T(8,128)S(1)} reduce(f32[32,256,256]{2,1,0:T(8,128)} %bitcast.52, f32[]{:T(128)} %constant.83.clone.1), dimensions={0}, to_apply=%region_0.0 | reduce | flops 2031616 | bytes 8650756 | tf_op jit(solution)/shard_map/reduce_sum | solution.py:23
  197.0 0.1 copy.9
  197.2 11.7 %cholesky.50 = f32[128,128]{1,0:T(8,128)S(1)} custom-call(f32[128,128]{1,0:T(8,128)S(1)} %cholesky.118), custom_call_target="Cholesky" | custom-call | tf_op jit(solution)/shard_map/jit(cholesky)/cholesky | solution.py:25
  209.0 9.8 %custom-call.16 = f32[1,128,128]{1,2,0:T(8,128)S(1)} custom-call(f32[1,128,128]{2,1,0:T(8,128)S(1)} %get-tuple-element.23), custom_call_target="InvertDiagBlocksLowerTriangular" | custom-call | tf_op jit(solution)/shard_map/jit(cholesky)/cholesky | solution.py:25
  218.8 0.2 constant_dynamic-update-slice_fusion.1
  219.0 0.3 convolution_subtract_fusion.2
  219.3 11.9 %cholesky.105 = f32[128,128]{1,0:T(8,128)S(1)} custom-call(f32[128,128]{1,0:T(8,128)S(1)} %convolution_subtract_fusion.2), custom_call_target="Cholesky" | custom-call | tf_op jit(solution)/shard_map/jit(cholesky)/cholesky | solution.py:25
  231.2 0.7 compare_reduce_fusion
  233.2 0.1 triangular_solve.72
  233.3 4.0 %while.1 = (s32[]{:T(128)}, f32[256,256]{1,0:T(8,128)S(1)}, s32[2,2]{1,0:T(2,128)S(1)}, f32[2,128,128]{2,1,0:T(8,128)S(1)}, s32[]{:T(128)}) while((s32[]{:T(128)}, f32[256,256]{1,0:T(8,128)S(1)}, s32[2,2]{1,0:T(2,128)S(1)}, f32[2,128,128]{2,1,0:T(8,128)S(1)}, s32[]{:T(128)}) %tuple.27), condition=%wide.while_cond, body=%wide.while_body.sunk | while | flops 2 | bytes 131189 | solution.py:26
  233.3 0.6 fusion.27
  233.9 1.4 bitcast_dynamic-update-slice_fusion.2
  235.3 0.6 fusion.27
  235.9 1.4 bitcast_dynamic-update-slice_fusion.2
  237.3 19.7 %custom-call.17 = f32[2,128,128]{1,2,0:T(8,128)S(1)} custom-call(f32[2,128,128]{2,1,0:T(8,128)S(1)} %get-tuple-element.9), custom_call_target="InvertDiagBlocksLowerTriangular" | custom-call | tf_op jit(solution)/shard_map/triangular_solve | solution.py:26
  256.9 2.0 fusion
  259.0 68.4 %all-reduce.3.cloned.1.call-done = f32[256,512]{1,0:T(8,128)} async-done(((f32[256,512]{1,0:T(8,128)}), f32[256,512]{1,0:T(8,128)}) %all-reduce.3.cloned.1.call-update) | async-done | bytes 524304 | tf_op jit(solution)/shard_map/psum | solution.py:21
  327.4 1.5 fusion.2
  328.9 1.3 convolution_subtract_fusion.1
  330.2 0.4 fusion.8
  330.6 0.8 pad_maximum_fusion.1
  331.5 1.0 convolution_subtract_fusion
  332.5 1.1 fusion.9
  333.5 1.5 pad_maximum_fusion
  (18 shorter events, 0.2 us)
Async XLA Ops:
  7.2 103.3 %copy-start = (f32[256,512]{1,0:T(8,128)S(1)}, f32[256,512]{1,0:T(8,128)}, u32[]{:S(2)}) copy-start(f32[256,512]{1,0:T(8,128)} %param.3) | copy-start | bytes 1572868
  7.2 185.9 %all-gather.3.cloned.1.call-start = ((), (), s32[]{:S(2)}) async-start(), calls=%async_computation.2 | async-start | bytes 8650752 | tf_op jit(solution)/shard_map/all_gather | solution.py:23
  110.5 3.7 %copy-start.1 = (f32[16,32,2048]{2,0,1:T(8,128)}, f32[16,32,2048]{2,0,1:T(8,128)S(1)}, u32[]{:S(2)}) copy-start(f32[16,32,2048]{2,0,1:T(8,128)S(1)} %all_to_all.19) | copy-start | bytes 12582916
  116.8 210.6 %all-reduce.3.cloned.1.call-start = ((), (), s32[]{:S(2)}) async-start(), calls=%async_computation.1 | async-start | bytes 1048576 | tf_op jit(solution)/shard_map/psum | solution.py:21
  327.4 4.1 %copy-start.2 = (f32[128,2048]{1,0:T(8,128)S(1)}, f32[128,2048]{1,0:T(8,128)}, u32[]{:S(2)}) copy-start(f32[128,2048]{1,0:T(8,128)} %fusion) | copy-start | bytes 3145732
Sparse Core Ops, SparseCore 0:
  116.9 76.0 all-gather.2
  198.9 128.4 all-reduce.2
